TPU v7x, 8 devices: a whole 2x2x1 slice. The times are simulated.
8 devices in a mesh: dp: 1 (over z), ep: 8 (over x, y, core).
Axes of the slice: x: 2, y: 2, z: 1, core: 2. Of those that a mesh axis runs over, the one named last changes fastest.
Arguments:
- x: bfloat16 [1, 8, 256, 7168], P('dp', 'ep')
- expert: int32 [1, 8, 256, 8], P('dp', 'ep')
- slot: int32 [1, 8, 256, 8], P('dp', 'ep')
- gate: float32 [1, 8, 256, 8], P('dp', 'ep')
- w_gate: bfloat16 [24, 7168, 2048], P('ep')
- w_up: bfloat16 [24, 7168, 2048], P('ep')
- w_down: bfloat16 [24, 2048, 7168], P('ep')
- s_gate: bfloat16 [7168, 2048], replicated
- s_up: bfloat16 [7168, 2048], replicated
- s_down: bfloat16 [2048, 7168], replicated
Outputs:
- y: bfloat16 [1, 8, 256, 7168], P('dp', 'ep')
All inputs are finite; a program needn't handle non-finite values.
Results may differ from a plain program's by a relative error of at most 0.009.
Values are sent between devices in bfloat16 or wider.
A program may use at most 2 GiB of HBM per device.

v0:
```python
import jax
import jax.numpy as jnp
from jax import lax
from jax.sharding import NamedSharding, PartitionSpec as P


def einsum(form, a, b):
    return jnp.einsum(form, a.astype(jnp.float32), b.astype(jnp.float32))


def for_all(x, s_gate, s_up, s_down):
    h = jax.nn.silu(einsum("...d,df->...f", x, s_gate)) * einsum("...d,df->...f", x, s_up)
    return einsum("...f,fd->...d", h.astype(jnp.bfloat16), s_down)


def solution(mesh):
    def placed(v, *spec):
        return lax.with_sharding_constraint(v, NamedSharding(mesh, P(*spec)))

    def step(x, expert, slot, gate, w_gate, w_up, w_down, s_gate, s_up, s_down):
        experts, (tokens, top) = w_gate.shape[0], expert.shape[2:]
        slots = 5 * tokens * top // (4 * experts)
        to_expert = jax.nn.one_hot(expert, experts, dtype=jnp.bfloat16)
        to_slot = jax.nn.one_hot(slot, slots, dtype=jnp.bfloat16)
        weighted = to_expert * gate[..., None].astype(jnp.bfloat16)
        dispatch = einsum("abtke,abtkc->abtec", to_expert, to_slot).astype(jnp.bfloat16)
        combine = einsum("abtke,abtkc->abtec", weighted, to_slot).astype(jnp.bfloat16)
        z = einsum("abtec,abtd->aebcd", dispatch, x).astype(jnp.bfloat16)
        z = placed(z, "dp", None, "ep", None, None)
        z = placed(z, "dp", "ep", None, None, None)
        h = jax.nn.silu(einsum("aebcd,edf->aebcf", z, w_gate))
        h = (h * einsum("aebcd,edf->aebcf", z, w_up)).astype(jnp.bfloat16)
        out = einsum("aebcf,efd->aebcd", h, w_down).astype(jnp.bfloat16)
        out = placed(out, "dp", "ep", None, None, None)
        out = placed(out, "dp", None, "ep", None, None)
        y = einsum("abtec,aebcd->abtd", combine, out)
        return (y + for_all(x, s_gate, s_up, s_down)).astype(jnp.bfloat16)

    return step
```

profile of v0, /device:TPU:0, one launch (start us, length us, event | category | flops | bytes accessed | tf_op | source)
XLA Modules:
  0.0 1211.5 jit_solution(6701494279065779758)
XLA Ops:
  0.0 0.8 copy.11
  0.8 0.0 copy-start.1
  0.8 0.8 copy.9
  1.7 0.0 copy-start.3
  1.7 2.8 convolution_convert_fusion.1
  4.5 18.5 %convolution_convert_fusion = bf16[24,106,7168]{2,1,0:T(8,128)(2,1)} fusion(bf16[1,1,256,7168]{3,2,1,0:T(8,128)(2,1)} %param.3, bf16[256,24,106]{2,1,0:T(8,128)(2,1)S(1)} %convolution_convert_fusion.1), kind=kOutput, calls=%fused_computation.11 | convolution fusion | flops 9354756096 | bytes 41443328 | tf_op jit(solution)/abtec,abtd->aebcd/dot_general | solution.py:8
  23.0 0.0 copy-done.1
  23.0 0.0 copy-done.3
  23.0 428.1 %all-to-all.4 = bf16[1,8,3,1,106,7168]{5,4,2,3,0,1:T(8,128)(2,1)} all-to-all(bf16[1,8,3,1,106,7168]{5,4,2,3,0,1:T(8,128)(2,1)} %bitcast.132), channel_id=1, replica_groups=mesh['dp'=1,'ep'=8] {'ep'}, dimensions={1} | all-to-all | bytes 72941568 | tf_op jit(solution)/sharding_constraint;jit(solution)/sharding_constraint | solution.py:18
  451.1 89.2 %fusion.2 = f32[3,8,106,2048]{3,2,1,0:T(8,128)} fusion(bf16[3,7168,2048]{2,1,0:T(8,128)(2,1)} %param.5, bf16[1,8,3,1,106,7168]{5,4,2,3,0,1:T(8,128)(2,1)} %all-to-all.4), kind=kOutput, calls=%fused_computation.2 | convolution fusion | flops 74692165632 | bytes 145391616 | tf_op jit(solution)/aebcd,edf->aebcf/dot_general | solution.py:8
  540.3 94.2 %fusion.12 = bf16[1,3,8,106,2048]{4,3,2,1,0:T(8,128)(2,1)} fusion(f32[3,8,106,2048]{3,2,1,0:T(8,128)} %fusion.2, bf16[3,7168,2048]{2,1,0:T(8,128)(2,1)} %param.4, bf16[1,8,3,1,106,7168]{5,4,2,3,0,1:T(8,128)(2,1)} %all-to-all.4), kind=kOutput, calls=%fused_computation.13 | convolution fusion | flops 74723426304 | bytes 155811840 | tf_op jit(solution)/aebcd,edf->aebcf/dot_general | solution.py:8
  634.5 87.7 %convert_bitcast_fusion = bf16[1,3,8,1,106,7168]{5,4,2,1,3,0:T(8,128)(2,1)} fusion(bf16[3,2048,7168]{2,1,0:T(8,128)(2,1)} %param.6, bf16[1,3,8,106,2048]{4,3,2,1,0:T(8,128)(2,1)} %fusion.12), kind=kOutput, calls=%fused_computation.8 | convolution fusion | flops 74710401024 | bytes 134971392 | tf_op jit(solution)/aebcf,efd->aebcd/dot_general | solution.py:8
  722.2 26.5 %copy.15 = bf16[1,3,8,1,106,7168]{5,4,1,3,0,2:T(8,128)(2,1)} copy(bf16[1,3,8,1,106,7168]{5,4,2,1,3,0:T(8,128)(2,1)} %convert_bitcast_fusion) | data formatting | bytes 72941568 | tf_op jit(solution)/sharding_constraint;jit(solution)/sharding_constraint | solution.py:18
  748.7 0.0 copy-start.5
  748.7 0.0 copy-start.2
  748.7 0.0 copy-start.4
  748.7 6.7 all-to-all-start.1
  755.3 0.0 copy-done.5
  755.4 0.1 copy.10
  755.5 0.0 copy-done.2
  755.5 0.0 copy-done.4
  755.5 2.9 convolution_convert_fusion.2
  758.4 0.0 copy-start
  758.4 14.5 %fusion.34 = f32[1,256,2048]{2,1,0:T(8,128)S(1)} fusion(bf16[7168,2048]{1,0:T(8,128)(2,1)} %param.7, bf16[1,1,256,7168]{3,2,1,0:T(8,128)(2,1)} %param.3), kind=kOutput, calls=%fused_computation.31 | convolution fusion | flops 7516192768 | bytes 35127296 | tf_op jit(solution)/...d,df->...f/dot_general | solution.py:8
  772.9 0.0 copy-done
  772.9 13.9 %fusion.40 = bf16[256,2048]{1,0:T(8,128)(2,1)S(1)} fusion(bf16[7168,2048]{1,0:T(8,128)(2,1)} %param.8, bf16[1,1,256,7168]{3,2,1,0:T(8,128)(2,1)S(1)} %copy-done, f32[1,256,2048]{2,1,0:T(8,128)S(1)} %fusion.34), kind=kOutput, calls=%fused_computation.33 | convolution fusion | flops 7519338496 | bytes 36175872 | tf_op jit(solution)/...d,df->...f/dot_general | solution.py:8
  786.9 384.4 %all-to-all-done.1 = bf16[1,3,8,1,106,7168]{5,4,1,3,0,2:T(8,128)(2,1)} async-done(((bf16[1,3,8,1,106,7168]{5,4,1,3,0,2:T(8,128)(2,1)}), bf16[1,3,8,1,106,7168]{5,4,1,3,0,2:T(8,128)(2,1)}, u32[]{:S(2)}, u32[]{:S(2)}) %all-to-all-start.1) | async-done | bytes 36470816 | tf_op jit(solution)/sharding_constraint;jit(solution)/sharding_constraint | solution.py:18
  1171.3 20.4 %convolution_bitcast_fusion = f32[256,7168]{1,0:T(8,128)} fusion(bf16[24,106,7168]{2,1,0:T(8,128)(2,1)} %bitcast.37, bf16[256,24,106]{2,1,0:T(8,128)(2,1)S(1)} %convolution_convert_fusion.2), kind=kOutput, calls=%fused_computation.20 | convolution fusion | flops 9336520704 | bytes 45113344 | tf_op jit(solution)/abtec,aebcd->abtd/dot_general | solution.py:8
  1191.7 19.8 %fusion.22 = bf16[1,1,256,7168]{3,2,1,0:T(8,128)(2,1)} fusion(f32[256,7168]{1,0:T(8,128)} %convolution_bitcast_fusion, bf16[256,2048]{1,0:T(8,128)(2,1)S(1)} %fusion.40, bf16[2048,7168]{1,0:T(8,128)(2,1)} %param.9), kind=kOutput, calls=%fused_computation.23 | convolution fusion | flops 7519862784 | bytes 41418752 | tf_op jit(solution)/...f,fd->...d/dot_general | solution.py:8
  (1 shorter events, 0.0 us)
Async XLA Ops:
  0.8 22.2 %copy-start.1 = (s32[256,8]{1,0:T(8,128)}, s32[256,8]{1,0:T(8,128)S(1)}, u32[]{:S(2)}) copy-start(s32[256,8]{1,0:T(8,128)S(1)} %copy.11) | copy-start | bytes 24580
  1.7 21.3 %copy-start.3 = (s32[256,8]{1,0:T(8,128)}, s32[256,8]{1,0:T(8,128)S(1)}, u32[]{:S(2)}) copy-start(s32[256,8]{1,0:T(8,128)S(1)} %copy.9) | copy-start | bytes 24580
  748.7 6.7 copy-start.5
  748.7 6.8 copy-start.2
  748.7 6.8 copy-start.4
  748.7 422.6 %all-to-all-start.1 = ((bf16[1,3,8,1,106,7168]{5,4,1,3,0,2:T(8,128)(2,1)}), bf16[1,3,8,1,106,7168]{5,4,1,3,0,2:T(8,128)(2,1)}, u32[]{:S(2)}, u32[]{:S(2)}) async-start(bf16[1,3,8,1,106,7168]{5,4,1,3,0,2:T(8,128)(2,1)} %copy.15), calls=%async_computation.1 | async-start | bytes 77070336 | tf_op jit(solution)/sharding_constraint;jit(solution)/sharding_constraint | solution.py:18
  758.4 14.5 %copy-start = (bf16[1,1,256,7168]{3,2,1,0:T(8,128)(2,1)S(1)}, bf16[1,1,256,7168]{3,2,1,0:T(8,128)(2,1)}, u32[]{:S(2)}) copy-start(bf16[1,1,256,7168]{3,2,1,0:T(8,128)(2,1)} %param.3) | copy-start | bytes 11010052
where the time goes:
time: 1210 us
  blocking collectives  428 us (35%)
  waiting for transfers between devices  384 us (32%)
  matrix products  364 us (30%)
  local copies, waits for them, and re-layouts  28.3 us (2%)
    another operation x1, blocking collectives, placed(): return lax.with_sharding_constraint(v, NamedSharding(mesh, P(*spec)))  428 us
    another operation x1, waiting for transfers between devices, placed(): return lax.with_sharding_constraint(v, NamedSharding(mesh, P(*spec)))  384 us
    dot_general x10, matrix products, einsum(): return jnp.einsum(form, a.astype(jnp.float32), b.astype(jnp.float32))  364 us
    another operation x1, local copies, waits for them, and re-layouts, placed(): return lax.with_sharding_constraint(v, NamedSharding(mesh, P(*spec)))  26.5 us
  transfers between devices with their start and end apart: 1, of which 1 were waited for; matrix products, arithmetic and copies ran while one was open for 3% of the time, Pallas kernels for 0%

commit v1 on v0

v1 whole, which is shorter than its diff:
```python
import functools

import jax
import jax.numpy as jnp
from jax import lax
from jax.experimental import pallas as pl
from jax.experimental.pallas import tpu as pltpu
from jax.sharding import PartitionSpec as P

F32, BF16 = jnp.float32, jnp.bfloat16
VMEM_LIMIT = 62 * 2**20
WIN = 112
TILE = 512


def dot(a, b):
    return lax.dot_general(a, b, (((a.ndim - 1,), (b.ndim - 2,)), ((), ())), preferred_element_type=F32)


def remote(src, dst, left, here, device):
    return pltpu.make_async_remote_copy(
        src_ref=src,
        dst_ref=dst,
        send_sem=left,
        recv_sem=here,
        device_id={"ep": device},
        device_id_type=pl.DeviceIdType.MESH,
    )


def others():
    me = lax.axis_index("ep")
    return me + 1 - 2 * (me % 2), me + 2 - 4 * ((me // 2) % 2), me + 4 - 8 * ((me // 4) % 2)


def meet(barrier, devices):
    for device in devices:
        pl.semaphore_signal(barrier, inc=1, device_id={"ep": device}, device_id_type=pl.DeviceIdType.MESH)
    pl.semaphore_wait(barrier, len(devices))


def dispatch(pos_ref, i, x_ref, z_ref, at):
    pos = pos_ref[pl.ds(i, 1), :]
    hot = (lax.broadcasted_iota(jnp.int32, (WIN, pos.shape[1]), 0) == pos).astype(F32).astype(BF16)
    for k in range(0, z_ref.shape[1], 512):
        z_ref[at : at + WIN, k : k + 512] = dot(hot, x_ref[:, k : k + 512]).astype(BF16)


def gather_kernel(own, n, plan, pos_ref, x_ref, sg_ref, su_ref, wg_ref, wu_ref, *refs):
    hs_ref, h_ref, g_ref, u_ref, far_ref, xp_ref, xr_ref, zp_ref, zr_ref, ga_ref, ua_ref = refs[:11]
    pair_left, pair_here, left, here = refs[11:]
    shared, pairs, rest, per = plan
    i = pl.program_id(0)
    depth = wg_ref.shape[1]
    half = x_ref.shape[0] // 2
    partner, beside_y, beside_x = others()
    barrier = pltpu.get_barrier_semaphore()

    def block(c, q):
        return xr_ref.at[q] if c == 0 else far_ref.at[q]

    def copy(c, k):
        if k < 2:
            src, dst, device = x_ref.at[:, pl.ds(c * depth, depth)], block(c, 2 * k), (beside_y, beside_x)[k]
        elif k == 2:
            src, dst, device = block(c, 2).at[pl.ds(0, half)], block(c, 4).at[pl.ds(0, half)], beside_y
        elif k == 3:
            src, dst, device = block(c, 0).at[pl.ds(half, half)], block(c, 4).at[pl.ds(half, half)], beside_x
        else:
            src, dst, device = block(c, 2 * k - 8), block(c, 2 * k - 7), partner
        return remote(src, dst, left.at[c, k], here.at[c, k], device)

    pair = remote(x_ref, xp_ref, pair_left.at[0], pair_here.at[0], partner)

    @pl.when(i == 0)
    def _():
        meet(barrier, (partner, beside_y, beside_x))
        copy(0, 0).start()
        copy(0, 1).start()
        pair.start()

    def forward(c):
        copy(c, 0).wait_recv()
        copy(c, 1).wait_recv()
        for k in (2, 3, 4, 5):
            copy(c, k).start()

    def onward(c):
        copy(c, 2).wait_recv()
        copy(c, 3).wait_recv()
        copy(c, 6).start()

    def arrived(c):
        for k in (4, 5, 6):
            copy(c, k).wait_recv()

    @pl.when(i == shared + 10)
    def _():
        forward(0)
        copy(1, 0).start()
        copy(1, 1).start()

    @pl.when(i == shared + 20)
    def _():
        onward(0)

    @pl.when(i == shared + pairs + 5)
    def _():
        forward(1)

    @pl.when(i == shared + pairs + 9)
    def _():
        onward(1)

    def two_halves(k, z_ref, ws, rows, cols, store):
        for part in range(2):

            @pl.when(k == part)
            def _():
                z = z_ref[:rows, part * depth : (part + 1) * depth]
                g, u = dot(z, ws[0]), dot(z, ws[1])
                if part == 0:
                    ga_ref[:rows, :cols] = g
                    ua_ref[:rows, :cols] = u
                else:
                    g, u = g + ga_ref[:rows, :cols], u + ua_ref[:rows, :cols]
                    store((jax.nn.silu(g) * u).astype(BF16))

    @pl.when(i < shared)
    def _():
        def store(v):
            hs_ref[...] = v

        two_halves(i % 2, x_ref, (sg_ref[...], su_ref[...]), x_ref.shape[0], sg_ref.shape[1], store)

    @pl.when((i >= shared) & (i < shared + pairs))
    def _():
        p = i - shared

        @pl.when(p == 0)
        def _():
            pair.wait_recv()

        @pl.when(p % (2 * per) == 0)
        def _():
            e = p // (2 * per)
            dispatch(pos_ref, e, x_ref, zp_ref, 0)
            dispatch(pos_ref, own + e, xp_ref, zp_ref, WIN)

        def store(v):
            h_ref[0] = v

        two_halves(p % 2, zp_ref, (wg_ref[0], wu_ref[0]), 2 * WIN, wg_ref.shape[2], store)

    @pl.when(i >= shared + pairs)
    def _():
        r = i - shared - pairs

        @pl.when(r == 0)
        def _():
            arrived(0)

        @pl.when(r % per == 0)
        def _():
            for q in range(n - 2):
                dispatch(pos_ref, (q + 2) * own + r // per, xr_ref.at[q], zr_ref, q * WIN)

        rows = zr_ref.shape[0] // 2
        for m in (0, rows):
            z = zr_ref[m : m + rows, :]
            g_ref[0, m : m + rows, :] = dot(z, wg_ref[0])
            u_ref[0, m : m + rows, :] = dot(z, wu_ref[0])

    @pl.when(i == shared + pairs + rest - 1)
    def _():
        arrived(1)
        pair.wait_send()
        for c in range(2):
            for k in range(7):
                copy(c, k).wait_send()


def gather(x, pos, s_gate, s_up, w_gate, w_up):
    tokens, depth = x.shape
    own, _, ff = w_gate.shape
    n = pos.shape[0] // own
    half = depth // 2
    per = ff // TILE
    narrow = TILE // 2
    shared, pairs, rest = 2 * s_gate.shape[1] // narrow, 2 * own * per, own * per
    rows = (n - 2) * WIN
    one = pl.Buffered(1)

    def whole(v):
        return pl.BlockSpec(v.shape, lambda i: (0,) * v.ndim, pipeline_mode=one)

    def s_at(i):
        i = jnp.minimum(i, shared - 1)
        return i % 2, i // 2

    def w_at(i):
        p = jnp.clip(i - shared, 0, pairs - 1)
        r = jnp.maximum(i - shared - pairs, 0)
        late = i >= shared + pairs
        return (
            jnp.where(late, r // per, p // (2 * per)),
            jnp.where(late, 0, p % 2),
            jnp.where(late, r % per, p // 2 % per),
        )

    def h_at(i):
        p = jnp.clip(i - shared, 0, pairs - 1)
        return p // (2 * per), 0, p // 2 % per

    def a_at(i):
        r = jnp.maximum(i - shared - pairs, 0)
        return r // per, 0, r % per

    s_spec = pl.BlockSpec((half, narrow), s_at)
    w_spec = pl.BlockSpec((1, half, TILE), w_at)
    a_spec = pl.BlockSpec((1, rows, TILE), a_at)
    wide = jax.ShapeDtypeStruct((own, rows, ff), F32)
    dma = pltpu.SemaphoreType.DMA
    flops = 4 * (tokens * s_gate.shape[1] + own * (2 * WIN + rows // 2) * ff) * depth
    return pl.pallas_call(
        functools.partial(gather_kernel, own, n, (shared, pairs, rest, per)),
        out_shape=(
            jax.ShapeDtypeStruct((tokens, s_gate.shape[1]), BF16),
            jax.ShapeDtypeStruct((own, 2 * WIN, ff), BF16),
            wide,
            wide,
            jax.ShapeDtypeStruct((n - 2, tokens, half), BF16),
        ),
        grid=(shared + pairs + rest,),
        in_specs=[whole(pos), whole(x), s_spec, s_spec, w_spec, w_spec],
        out_specs=(
            pl.BlockSpec((tokens, narrow), lambda i: (0, jnp.minimum(i, shared - 1) // 2)),
            pl.BlockSpec((1, 2 * WIN, TILE), h_at),
            a_spec,
            a_spec,
            pl.BlockSpec(memory_space=pl.ANY),
        ),
        scratch_shapes=[
            pltpu.VMEM((tokens, depth), BF16),
            pltpu.VMEM((n - 2, tokens, half), BF16),
            pltpu.VMEM((2 * WIN, depth), BF16),
            pltpu.VMEM((rows, half), BF16),
            pltpu.VMEM((tokens, TILE), F32),
            pltpu.VMEM((tokens, TILE), F32),
            dma((1,)),
            dma((1,)),
            dma((2, 7)),
            dma((2, 7)),
        ],
        compiler_params=pltpu.CompilerParams(
            vmem_limit_bytes=VMEM_LIMIT, collective_id=1, has_side_effects=True
        ),
        cost_estimate=pl.CostEstimate(flops=flops, bytes_accessed=own * 2 * depth * ff * 2, transcendentals=0),
        name="gather",
    )(pos, x, s_gate, s_up, w_gate, w_up)


def rest_kernel(own, pos_ref, x_ref, wg_ref, wu_ref, g_ref, u_ref, h_ref, z_ref):
    e = pl.program_id(0)

    @pl.when(pl.program_id(1) == 0)
    def _():
        for q in range(x_ref.shape[0]):
            dispatch(pos_ref, (q + 2) * own + e, x_ref.at[q], z_ref, q * WIN)

    rows = z_ref.shape[0] // 2
    for m in (0, rows):
        z = z_ref[m : m + rows, :]
        g = dot(z, wg_ref[0]) + g_ref[0, m : m + rows, :]
        u = dot(z, wu_ref[0]) + u_ref[0, m : m + rows, :]
        h_ref[0, m : m + rows, :] = (jax.nn.silu(g) * u).astype(BF16)


def finish(pos, x, w_gate, w_up, g, u):
    own, rows, ff = g.shape
    half = x.shape[2]
    one = pl.Buffered(1)

    def whole(v):
        return pl.BlockSpec(v.shape, lambda e, j: (0,) * v.ndim, pipeline_mode=one)

    w_spec = pl.BlockSpec((1, half, TILE), lambda e, j: (e, 1, j))
    a_spec = pl.BlockSpec((1, rows, TILE), lambda e, j: (e, 0, j))
    return pl.pallas_call(
        functools.partial(rest_kernel, own),
        out_shape=jax.ShapeDtypeStruct((own, rows, ff), BF16),
        grid=(own, ff // TILE),
        in_specs=[whole(pos), whole(x), w_spec, w_spec, a_spec, a_spec],
        out_specs=a_spec,
        scratch_shapes=[pltpu.VMEM((rows, half), BF16)],
        compiler_params=pltpu.CompilerParams(vmem_limit_bytes=VMEM_LIMIT),
        cost_estimate=pl.CostEstimate(
            flops=4 * own * rows * half * ff, bytes_accessed=4 * own * half * ff, transcendentals=0
        ),
        name="finish",
    )(pos, x, w_gate, w_up, g, u)


def down_kernel(n, own, tiles, pos_ref, gate_ref, here_ref, away_ref, hs_ref, w_ref, s_ref, y_ref, out_ref, mix_ref, *bufs):
    pair_out, pair_in, far_out, far_in, near_out, near_in = bufs[:6]
    pair_left, pair_here, far_left, far_here, near_left, near_here = bufs[6:]
    tokens = pos_ref.shape[0]
    rows = out_ref.shape[2]
    half = tokens // 2
    j = pl.program_id(0)
    partner, beside_y, beside_x = others()
    barrier = pltpu.get_barrier_semaphore()

    def pair(i):
        return remote(pair_out.at[i % 2], pair_in.at[i % 6], pair_left.at[i % 2], pair_here.at[i % 6], partner)

    def far(i, k):
        part = far_out.at[i % 2, k]
        return remote(part, far_in.at[i % 4, k], far_left.at[i % 2, k], far_here.at[i % 4, k], (beside_x, beside_y)[k])

    def near(i, k):
        part = near_out.at[i % 2, k]
        return remote(part, near_in.at[i % 4, k], near_left.at[i % 2, k], near_here.at[i % 4, k], (beside_x, beside_y)[k])

    def term(i, b):
        seen = [out_ref[i % 4, e, b * WIN : (b + 1) * WIN, :] for e in range(own)]
        return dot(mix_ref[b], jnp.concatenate(seen, axis=0))

    @pl.when(j == 0)
    def _():
        lane = lax.broadcasted_iota(jnp.int32, (tokens, WIN), 1)
        for b in range(n):
            for e in range(own):
                i = b * own + e
                hit = pos_ref[:, i : i + 1] == lane
                mix_ref[b, :, e * WIN : (e + 1) * WIN] = jnp.where(hit, gate_ref[:, i : i + 1], 0.0).astype(BF16)
        meet(barrier, (partner, beside_y, beside_x))

    @pl.when(j < tiles)
    def _():
        for e in range(own):
            out_ref[j % 4, e, : 2 * WIN, :] = dot(here_ref[e], w_ref[e]).astype(BF16)
            step = (rows - 2 * WIN) // 2
            for r in (0, step):
                at = 2 * WIN + r
                out_ref[j % 4, e, at : at + step, :] = dot(away_ref[e, r : r + step, :], w_ref[e]).astype(BF16)

        @pl.when(j >= 2)
        def _():
            pair(j - 2).wait_send()

        for q in range(n // 2):
            pair_out[j % 2, q] = term(j, 2 * q + 1).astype(BF16)
        pair(j).start()

    @pl.when((j >= 1) & (j <= tiles))
    def _():
        i = j - 1
        pair(i).wait_recv()

        @pl.when(i >= 2)
        def _():
            far(i - 2, 0).wait_send()
            far(i - 2, 1).wait_send()

        total = (term(i, 6) + pair_in[i % 6, 3].astype(F32)).astype(BF16)
        far_out[i % 2, 0] = total[:half]
        far_out[i % 2, 1] = total[half:]
        far(i, 0).start()
        far(i, 1).start()

    @pl.when((j >= 2) & (j <= tiles + 1))
    def _():
        i = j - 2
        far(i, 0).wait_recv()
        far(i, 1).wait_recv()

        @pl.when(i >= 2)
        def _():
            near(i - 2, 0).wait_send()
            near(i - 2, 1).wait_send()

        total = term(i, 4) + pair_in[i % 6, 2].astype(F32)
        near_out[i % 2, 0, :half] = total[:half].astype(BF16)
        near_out[i % 2, 0, half:] = (total[half:] + far_in[i % 4, 1].astype(F32)).astype(BF16)
        near(i, 0).start()
        total = term(i, 2) + pair_in[i % 6, 1].astype(F32)
        near_out[i % 2, 1, :half] = (total[:half] + far_in[i % 4, 0].astype(F32)).astype(BF16)
        near_out[i % 2, 1, half:] = total[half:].astype(BF16)
        near(i, 1).start()

    @pl.when(j >= 3)
    def _():
        i = j - 3
        total = dot(hs_ref[...], s_ref[...]) + term(i, 0) + pair_in[i % 6, 0].astype(F32)
        near(i, 0).wait_recv()
        near(i, 1).wait_recv()
        total = total + near_in[i % 4, 0].astype(F32) + near_in[i % 4, 1].astype(F32)
        y_ref[...] = total.astype(BF16)

    @pl.when(j == tiles + 2)
    def _():
        for i in (tiles - 2, tiles - 1):
            pair(i).wait_send()
            for k in range(2):
                far(i, k).wait_send()
                near(i, k).wait_send()


def down(here, away, hs, w_down, s_down, pos, gate, tile):
    own, _, ff = here.shape
    n = pos.shape[1] // own
    rows = n * WIN
    tokens, depth = pos.shape[0], w_down.shape[2]
    tiles = depth // tile
    half = tokens // 2
    one = pl.Buffered(1)

    def whole(v):
        return pl.BlockSpec(v.shape, lambda j: (0,) * v.ndim, pipeline_mode=one)

    flops = 2 * own * rows * ff * depth
    dma = pltpu.SemaphoreType.DMA
    return pl.pallas_call(
        functools.partial(down_kernel, n, own, tiles),
        out_shape=jax.ShapeDtypeStruct((tokens, depth), BF16),
        grid=(tiles + 3,),
        in_specs=[
            whole(pos),
            whole(gate),
            whole(here),
            whole(away),
            whole(hs),
            pl.BlockSpec((own, ff, tile), lambda j: (0, 0, jnp.minimum(j, tiles - 1))),
            pl.BlockSpec((s_down.shape[0], tile), lambda j: (0, jnp.maximum(j - 3, 0))),
        ],
        out_specs=pl.BlockSpec((tokens, tile), lambda j: (0, jnp.maximum(j - 3, 0))),
        scratch_shapes=[
            pltpu.VMEM((4, own, rows, tile), BF16),
            pltpu.VMEM((n, tokens, own * WIN), BF16),
            pltpu.VMEM((2, n // 2, tokens, tile), BF16),
            pltpu.VMEM((6, n // 2, tokens, tile), BF16),
            pltpu.VMEM((2, 2, half, tile), BF16),
            pltpu.VMEM((4, 2, half, tile), BF16),
            pltpu.VMEM((2, 2, tokens, tile), BF16),
            pltpu.VMEM((4, 2, tokens, tile), BF16),
            dma((2,)),
            dma((6,)),
            dma((2, 2)),
            dma((4, 2)),
            dma((2, 2)),
            dma((4, 2)),
        ],
        compiler_params=pltpu.CompilerParams(
            vmem_limit_bytes=VMEM_LIMIT, collective_id=0, has_side_effects=True
        ),
        cost_estimate=pl.CostEstimate(flops=flops, bytes_accessed=own * ff * depth * 2, transcendentals=0),
        name="down",
    )(pos, gate, here, away, hs, w_down, s_down)


def solution(mesh):
    n = mesh.shape["ep"]

    def local(x, expert, slot, gate, w_gate, w_up, w_down, s_gate, s_up, s_down):
        me = lax.axis_index("ep")
        x, expert, slot, gate = x[0, 0], expert[0, 0], slot[0, 0], gate[0, 0]
        tokens, top = expert.shape
        own = w_gate.shape[0]
        experts = own * n
        slots = 5 * tokens * top // (4 * experts)

        hit = (expert[:, :, None] == jnp.arange(experts)) & (slot < slots)[:, :, None]
        pos = jnp.sum(jnp.where(hit, slot[:, :, None] + 1, 0), axis=1) - 1
        weight = jnp.sum(jnp.where(hit, gate.astype(BF16).astype(F32)[:, :, None], 0.0), axis=1)
        both = lax.all_gather(jnp.concatenate([pos.astype(F32), weight], axis=1), "ep")
        both = both.reshape(n, tokens, 2, n, own)
        both = lax.dynamic_index_in_dim(both, me, 3, keepdims=False)
        both = both[me ^ jnp.arange(n)]
        pos = both[:, :, 0].astype(jnp.int32)
        weight = both[:, :, 1]
        pos_row = pos.transpose(0, 2, 1).reshape(n * own, tokens)
        pos_col = pos.transpose(1, 0, 2).reshape(tokens, n * own)
        weight = weight.transpose(1, 0, 2).reshape(tokens, n * own)

        hs, here, g, u, far = gather(x, pos_row, s_gate, s_up, w_gate, w_up)
        away = finish(pos_row, far, w_gate, w_up, g, u)
        y = down(here, away, hs, w_down, s_down, pos_col, weight, 512)
        return y[None, None]

    tok, exp, rep = P("dp", "ep"), P("ep"), P()
    return jax.shard_map(
        local,
        mesh=mesh,
        in_specs=(tok, tok, tok, tok, exp, exp, exp, rep, rep, rep),
        out_specs=tok,
        check_vma=False,
    )
```

time: 1210 us -> 432 us (0.36)
  blocking collectives: 428 us -> 15.3 us
  Pallas kernels: 0 us -> 405 us
  waiting for transfers between devices: 384 us -> 0 us
  matrix products: 364 us -> 0 us
  local copies, waits for them, and re-layouts: 28.3 us -> 7.11 us
    another operation x1 -> x0, blocking collectives: 428 us -> none  [placed(): return lax.with_sharding_constraint(v, NamedSharding(mesh, P(*spec)))]
    pallas_call x0 -> x3, Pallas kernels: none -> 405 us  [the longest x1 179 us: gather(): pl.pallas_call(functools.partial(gather_kernel, own, n, (shared, pairs, r...]
    another operation x1 -> x0, waiting for transfers between devices: 384 us -> none  [placed(): return lax.with_sharding_constraint(v, NamedSharding(mesh, P(*spec)))]
    dot_general x10 -> x0, matrix products: 364 us -> none  [einsum(): return jnp.einsum(form, a.astype(jnp.float32), b.astype(jnp.float32))]
    another operation x1 -> x0, local copies, waits for them, and re-layouts: 26.5 us -> none  [placed(): return lax.with_sharding_constraint(v, NamedSharding(mesh, P(*spec)))]
    all_gather x0 -> x1, blocking collectives: none -> 15.3 us  [local(): lax.all_gather(jnp.concatenate([pos.astype(F32), weight], axis=1), 'ep')]
  transfers between devices with their start and end apart: 1 -> 0, of which waited for: 1 -> 0; matrix products, arithmetic and copies ran while one was open for 3% -> 0% of each run, Pallas kernels for 0% -> 0%
where the time goes in v1:
time: 432 us
  Pallas kernels  405 us (94%)
  blocking collectives  15.3 us (4%)
  local copies, waits for them, and re-layouts  7.11 us (2%)
    pallas_call x1, Pallas kernels, gather(): pl.pallas_call(functools.partial(gather_kernel, own, n, (shared, pairs, r...  179 us
    pallas_call x1, Pallas kernels, down(): pl.pallas_call(functools.partial(down_kernel, n, own, tiles), out_shape=j...  149 us
    pallas_call x1, Pallas kernels, finish(): pl.pallas_call(functools.partial(rest_kernel, own), out_shape=jax.ShapeDt...  76.8 us
    all_gather x1, blocking collectives, local(): lax.all_gather(jnp.concatenate([pos.astype(F32), weight], axis=1), 'ep')  15.3 us

profile of v1, /device:TPU:0, one launch (start us, length us, event | category | flops | bytes accessed | tf_op | source)
XLA Modules:
  0.0 431.7 jit_solution(7011962536981282032)
XLA Ops:
  0.0 0.7 compare_bitcast_fusion
  0.7 0.7 add_bitcast_fusion
  1.4 0.7 select_reduce_fusion.1
  2.2 0.7 bitcast_convert_fusion
  2.9 0.7 select_reduce_fusion
  3.6 15.3 %all-gather = f32[2048,48]{0,1:T(8,128)S(1)} all-gather(f32[256,48]{0,1:T(8,128)S(1)} %pad_maximum_fusion), channel_id=2, replica_groups=mesh['dp'=1,'ep'=8] {'ep'}, dimensions={0}, use_global_device_ids=true | all-gather | bytes 442368 | tf_op jit(solution)/shard_map/all_gather | solution.py:476
  18.9 0.1 copy.52
  19.2 0.6 gather_fusion
  19.8 0.6 fusion.2
  20.5 0.6 reshape.58.pos_ref
  21.1 178.9 %gather.7 = (bf16[256,2048]{1,0:T(8,128)(2,1)}, bf16[3,224,2048]{2,1,0:T(8,128)(2,1)}, f32[3,672,2048]{2,1,0:T(8,128)}, f32[3,672,2048]{2,1,0:T(8,128)}, bf16[6,256,3584]{2,1,0:T(8,128)(2,1)}) custom-call(s32[24,256]{1,0:T(8,128)} %reshape.58.pos_ref, bf16[256,7168]{1,0:T(8,128)(2,1)} %bitcast.41, bf16[7168,2048]{1,0:T(8,128)(2,1)} %sg_ref.1, ...), custom_call_target="tpu_custom_call" | custom-call | flops 113682415616 | bytes 176160768 | tf_op jit(solution)/shard_map/gather/pallas_call | solution.py:225
  200.0 0.0 copy-start.1
  200.0 0.0 copy-start
  200.0 76.8 %finish.1.away_ref = bf16[3,672,2048]{2,1,0:T(8,128)(2,1)} custom-call(s32[24,256]{1,0:T(8,128)} %reshape.58.pos_ref, bf16[6,256,3584]{2,1,0:T(8,128)(2,1)} %get-tuple-element.11.x_ref, bf16[3,7168,2048]{2,1,0:T(8,128)(2,1)} %wg_ref.3, bf16[3,7168,2048]{2,1,0:T(8,128)(2,1)} %wu_ref.3, f32[3,672,2048]{2,1,0:T(8,128)} %get-tuple-element.12.g_ref, ...), custom_call_target="tpu_custom_call" | custom-call | flops 59190018048 | bytes 88080384 | tf_op jit(solution)/shard_map/finish/pallas_call | solution.py:289
  276.8 0.0 copy-done.1
  276.8 0.8 copy.49.pos_ref
  277.6 0.0 copy-done
  277.6 0.7 copy.50.gate_ref
  278.4 149.3 %down.1 = bf16[256,7168]{1,0:T(8,128)(2,1)} custom-call(s32[256,24]{1,0:T(8,128)} %copy.49.pos_ref, f32[256,24]{1,0:T(8,128)} %copy.50.gate_ref, bf16[3,224,2048]{2,1,0:T(8,128)(2,1)} %get-tuple-element.10.here_ref, bf16[3,672,2048]{2,1,0:T(8,128)(2,1)} %finish.1.away_ref, bf16[256,2048]{1,0:T(8,128)(2,1)} %get-tuple-element.14.hs_ref, ...), custom_call_target="tpu_custom_call" | custom-call | flops 78920024064 | bytes 88080384 | tf_op jit(solution)/shard_map/down/pallas_call | solution.py:424
  427.6 4.1 copy.62
  (12 shorter events, 0.2 us)
Async XLA Ops:
  200.0 76.8 %copy-start.1 = (s32[256,8,3]{0,1,2:T(8,128)S(1)}, s32[256,8,3]{0,1,2:T(8,128)}, u32[]{:S(2)}) copy-start(s32[256,8,3]{0,1,2:T(8,128)} %get-tuple-element.18) | copy-start | bytes 73732
  200.0 77.6 %copy-start = (f32[256,8,3]{0,1,2:T(8,128)S(1)}, f32[256,8,3]{0,1,2:T(8,128)}, u32[]{:S(2)}) copy-start(f32[256,8,3]{0,1,2:T(8,128)} %get-tuple-element.19) | copy-start | bytes 73732

commit v2 on v1

v2 whole, which is shorter than its diff:
```python
import functools

import jax
import jax.numpy as jnp
from jax import lax
from jax.experimental import pallas as pl
from jax.experimental.pallas import tpu as pltpu
from jax.sharding import PartitionSpec as P

F32, BF16 = jnp.float32, jnp.bfloat16
VMEM_LIMIT = 62 * 2**20
WIN = 112
TILE = 512
RING = 3


def dot(a, b):
    return lax.dot_general(a, b, (((a.ndim - 1,), (b.ndim - 2,)), ((), ())), preferred_element_type=F32)


def remote(src, dst, left, here, device):
    return pltpu.make_async_remote_copy(
        src_ref=src,
        dst_ref=dst,
        send_sem=left,
        recv_sem=here,
        device_id={"ep": device},
        device_id_type=pl.DeviceIdType.MESH,
    )


def others():
    me = lax.axis_index("ep")
    return me + 1 - 2 * (me % 2), me + 2 - 4 * ((me // 2) % 2), me + 4 - 8 * ((me // 4) % 2)


def flip(index, bits):
    for bit in (1, 2, 4):
        if bits & bit:
            index = index + bit - 2 * bit * ((index // bit) % 2)
    return index


def meet(barrier, devices):
    for device in devices:
        pl.semaphore_signal(barrier, inc=1, device_id={"ep": device}, device_id_type=pl.DeviceIdType.MESH)
    pl.semaphore_wait(barrier, len(devices))


def up_kernel(own, n, plan, note_ref, x_ref, sg_ref, su_ref, wg_ref, wu_ref, *refs):
    hs_ref, here_ref, away_ref, out_ref, far_ref, acc_ref = refs[:6]
    ring_ref, notes_ref, xp_ref, xr_ref, zp_ref, zr_ref, ga_ref, ua_ref, wide_ref = refs[6:15]
    note_left, note_here, pair_left, pair_here, left, here, ring_sem, load_sem, acc_sem = refs[15:]
    shared, pairs, rest, per = plan
    t = pl.program_id(0)
    depth = ring_ref.shape[2]
    half = x_ref.shape[0] // 2
    me = lax.axis_index("ep")
    partner, beside_y, beside_x = others()
    barrier = pltpu.get_barrier_semaphore()
    late = shared + pairs

    def block(c, q):
        return xr_ref.at[q] if c == 0 else far_ref.at[q]

    def copy(c, k):
        if k < 2:
            src, dst, device = x_ref.at[:, pl.ds(c * depth, depth)], block(c, 2 * k), (beside_y, beside_x)[k]
        elif k == 2:
            src, dst, device = block(c, 2).at[pl.ds(0, half)], block(c, 4).at[pl.ds(0, half)], beside_y
        elif k == 3:
            src, dst, device = block(c, 0).at[pl.ds(half, half)], block(c, 4).at[pl.ds(half, half)], beside_x
        else:
            src, dst, device = block(c, 2 * k - 8), block(c, 2 * k - 7), partner
        return remote(src, dst, left.at[c, k], here.at[c, k], device)

    pair = remote(x_ref, xp_ref, pair_left.at[0], pair_here.at[0], partner)

    def note(b):
        device = flip(me, b)
        return remote(note_ref.at[device], notes_ref.at[b], note_left.at[b], note_here.at[b], device)

    def weights(s, src, k, g):
        slot = s % RING
        return pltpu.make_async_copy(src, ring_ref.at[slot, g], ring_sem.at[slot, g])

    def fetch(s):
        @pl.when(s < shared)
        def _():
            at = pl.ds((s % 2) * depth, depth), pl.ds((s // 2) * TILE, TILE)
            for g, ref in enumerate((sg_ref, su_ref)):
                weights(s, ref.at[at], s % 2, g).start()

        @pl.when((s >= shared) & (s < late))
        def _():
            p = s - shared
            at = p // (2 * per), pl.ds((p % 2) * depth, depth), pl.ds((p // 2 % per) * TILE, TILE)
            for g, ref in enumerate((wg_ref, wu_ref)):
                weights(s, ref.at[at], p % 2, g).start()

        @pl.when((s >= late) & (s < late + 2 * rest))
        def _():
            r = (s - late) % rest
            k = (s - late) // rest
            at = r // per, pl.ds(k * depth, depth), pl.ds((r % per) * TILE, TILE)
            for g, ref in enumerate((wg_ref, wu_ref)):
                weights(s, ref.at[at], k, g).start()

    def load(q):
        return pltpu.make_async_copy(far_ref.at[q], xr_ref.at[q], load_sem.at[q])

    def spill(r):
        return pltpu.make_async_copy(wide_ref.at[r % 2], acc_ref.at[r], acc_sem.at[r % 2])

    def refill(r):
        return pltpu.make_async_copy(acc_ref.at[r], wide_ref.at[r % 2], acc_sem.at[r % 2])

    @pl.when(t == 0)
    def _():
        for s in range(RING):
            fetch(s)
        notes_ref[0] = note_ref[me]
        meet(barrier, [flip(me, b) for b in range(1, n)])
        for b in range(1, n):
            note(b).start()
        copy(0, 0).start()
        copy(0, 1).start()
        pair.start()

    def forward(c):
        copy(c, 0).wait_recv()
        copy(c, 1).wait_recv()
        for k in (2, 3, 4, 5):
            copy(c, k).start()

    def onward(c):
        copy(c, 2).wait_recv()
        copy(c, 3).wait_recv()
        copy(c, 6).start()

    def arrived(c):
        for k in (4, 5, 6):
            copy(c, k).wait_recv()

    @pl.when(t == shared + 10)
    def _():
        forward(0)
        copy(1, 0).start()
        copy(1, 1).start()

    @pl.when(t == shared + 20)
    def _():
        onward(0)

    @pl.when(t == late + 6)
    def _():
        forward(1)

    @pl.when(t == late + 10)
    def _():
        onward(1)

    @pl.when(t == late + rest - 1)
    def _():
        arrived(1)
        for k in range(2, 7):
            copy(0, k).wait_send()
        for q in range(n - 2):
            load(q).start()

    for g in range(2):
        weights(t, wg_ref.at[0, pl.ds(0, depth), pl.ds(0, TILE)], 0, g).wait()
    wg, wu = ring_ref.at[t % RING, 0], ring_ref.at[t % RING, 1]

    def two_halves(k, z_ref, rows, store):
        for part in range(2):

            @pl.when(k == part)
            def _():
                z = z_ref[:rows, part * depth : (part + 1) * depth]
                g, u = dot(z, wg[...]), dot(z, wu[...])
                if part == 0:
                    ga_ref[:rows] = g
                    ua_ref[:rows] = u
                else:
                    g, u = g + ga_ref[:rows], u + ua_ref[:rows]
                    store((jax.nn.silu(g) * u).astype(BF16))

    @pl.when(t < shared)
    def _():
        def store(v):
            hs_ref[...] = v

        two_halves(t % 2, x_ref, x_ref.shape[0], store)

    @pl.when((t >= shared) & (t < late))
    def _():
        p = t - shared

        @pl.when(p == 0)
        def _():
            pair.wait_recv()
            note(1).wait_recv()

        @pl.when(p % (2 * per) == 0)
        def _():
            e = p // (2 * per)
            dispatch(notes_ref, 0, e, x_ref, zp_ref, 0)
            dispatch(notes_ref, 1, e, xp_ref, zp_ref, WIN)

        def store(v):
            here_ref[0] = v

        two_halves(p % 2, zp_ref, 2 * WIN, store)

    @pl.when(t >= late)
    def _():
        r = (t - late) % rest
        k = (t - late) // rest

        @pl.when(t == late)
        def _():
            arrived(0)
            for b in range(2, n):
                note(b).wait_recv()
            out_ref[...] = notes_ref[...]

        @pl.when(t == late + rest)
        def _():
            for q in range(n - 2):
                load(q).wait()
            for i in (rest - 2, rest - 1):
                spill(i).wait()
            for i in (0, 1):
                refill(i).start()

        @pl.when(r % per == 0)
        def _():
            for q in range(n - 2):
                dispatch(notes_ref, q + 2, r // per, xr_ref.at[q], zr_ref, q * WIN)

        rows = zr_ref.shape[0] // 2

        @pl.when(k == 0)
        def _():
            @pl.when(r >= 2)
            def _():
                spill(r - 2).wait()

            for m in (0, rows):
                z = zr_ref[m : m + rows, :]
                wide_ref[r % 2, 0, m : m + rows, :] = dot(z, wg[...])
                wide_ref[r % 2, 1, m : m + rows, :] = dot(z, wu[...])
            spill(r).start()

        @pl.when(k == 1)
        def _():
            refill(r).wait()
            for m in (0, rows):
                z = zr_ref[m : m + rows, :]
                g = dot(z, wg[...]) + wide_ref[r % 2, 0, m : m + rows, :]
                u = dot(z, wu[...]) + wide_ref[r % 2, 1, m : m + rows, :]
                away_ref[0, m : m + rows, :] = (jax.nn.silu(g) * u).astype(BF16)

            @pl.when(r < rest - 2)
            def _():
                refill(r + 2).start()

    fetch(t + RING)

    @pl.when(t == late + 2 * rest - 1)
    def _():
        pair.wait_send()
        for b in range(1, n):
            note(b).wait_send()
        for k in range(7):
            if k < 2:
                copy(0, k).wait_send()
            copy(1, k).wait_send()


def dispatch(notes_ref, b, e, x_ref, z_ref, at):
    pos = notes_ref[b, pl.ds(e, 1), :]
    slot = lax.broadcasted_iota(jnp.int32, (WIN, pos.shape[1]), 0).astype(F32)
    hot = (slot == pos).astype(F32).astype(BF16)
    for k in range(0, z_ref.shape[1], 512):
        z_ref[at : at + WIN, k : k + 512] = dot(hot, x_ref[:, k : k + 512]).astype(BF16)


def up(x, note, s_gate, s_up, w_gate, w_up):
    tokens, depth = x.shape
    own, _, ff = w_gate.shape
    n = note.shape[0]
    half = depth // 2
    per = ff // TILE
    shared, pairs, rest = 2 * s_gate.shape[1] // TILE, 2 * own * per, own * per
    late = shared + pairs
    rows = (n - 2) * WIN
    one = pl.Buffered(1)

    def whole(v):
        return pl.BlockSpec(v.shape, lambda t: (0,) * v.ndim, pipeline_mode=one)

    def here_at(t):
        p = jnp.clip(t - shared, 0, pairs - 1)
        return p // (2 * per), 0, p // 2 % per

    def away_at(t):
        r = jnp.maximum(t - late - rest, 0)
        return r // per, 0, r % per

    anywhere = pl.BlockSpec(memory_space=pl.ANY)
    dma = pltpu.SemaphoreType.DMA
    flops = 4 * (tokens * s_gate.shape[1] + own * (2 * WIN + rows) * ff) * depth
    return pl.pallas_call(
        functools.partial(up_kernel, own, n, (shared, pairs, rest, per)),
        out_shape=(
            jax.ShapeDtypeStruct((tokens, s_gate.shape[1]), BF16),
            jax.ShapeDtypeStruct((own, 2 * WIN, ff), BF16),
            jax.ShapeDtypeStruct((own, rows, ff), BF16),
            jax.ShapeDtypeStruct(note.shape, F32),
            jax.ShapeDtypeStruct((n - 2, tokens, half), BF16),
            jax.ShapeDtypeStruct((rest, 2, rows, TILE), F32),
        ),
        grid=(late + 2 * rest,),
        in_specs=[whole(note), whole(x)] + [anywhere] * 4,
        out_specs=(
            pl.BlockSpec((tokens, TILE), lambda t: (0, jnp.minimum(t, shared - 1) // 2)),
            pl.BlockSpec((1, 2 * WIN, TILE), here_at),
            pl.BlockSpec((1, rows, TILE), away_at),
            whole(note),
            anywhere,
            anywhere,
        ),
        scratch_shapes=[
            pltpu.VMEM((RING, 2, half, TILE), BF16),
            pltpu.VMEM(note.shape, F32),
            pltpu.VMEM((tokens, depth), BF16),
            pltpu.VMEM((n - 2, tokens, half), BF16),
            pltpu.VMEM((2 * WIN, depth), BF16),
            pltpu.VMEM((rows, half), BF16),
            pltpu.VMEM((tokens, TILE), F32),
            pltpu.VMEM((tokens, TILE), F32),
            pltpu.VMEM((2, 2, rows, TILE), F32),
            dma((n,)),
            dma((n,)),
            dma((1,)),
            dma((1,)),
            dma((2, 7)),
            dma((2, 7)),
            dma((RING, 2)),
            dma((n - 2,)),
            dma((2,)),
        ],
        compiler_params=pltpu.CompilerParams(
            vmem_limit_bytes=VMEM_LIMIT, collective_id=1, has_side_effects=True
        ),
        cost_estimate=pl.CostEstimate(flops=flops, bytes_accessed=own * 4 * depth * ff * 2, transcendentals=0),
        name="up",
    )(note, x, s_gate, s_up, w_gate, w_up)[:4]


def down_kernel(n, own, tiles, pos_ref, gate_ref, here_ref, away_ref, hs_ref, w_ref, s_ref, y_ref, out_ref, mix_ref, *bufs):
    pair_out, pair_in, far_out, far_in, near_out, near_in = bufs[:6]
    pair_left, pair_here, far_left, far_here, near_left, near_here = bufs[6:]
    tokens = pos_ref.shape[0]
    rows = out_ref.shape[2]
    half = tokens // 2
    j = pl.program_id(0)
    partner, beside_y, beside_x = others()
    barrier = pltpu.get_barrier_semaphore()

    def pair(i):
        return remote(pair_out.at[i % 2], pair_in.at[i % 6], pair_left.at[i % 2], pair_here.at[i % 6], partner)

    def far(i, k):
        part = far_out.at[i % 2, k]
        return remote(part, far_in.at[i % 4, k], far_left.at[i % 2, k], far_here.at[i % 4, k], (beside_x, beside_y)[k])

    def near(i, k):
        part = near_out.at[i % 2, k]
        return remote(part, near_in.at[i % 4, k], near_left.at[i % 2, k], near_here.at[i % 4, k], (beside_x, beside_y)[k])

    def term(i, b):
        seen = [out_ref[i % 4, e, b * WIN : (b + 1) * WIN, :] for e in range(own)]
        return dot(mix_ref[b], jnp.concatenate(seen, axis=0))

    @pl.when(j == 0)
    def _():
        lane = lax.broadcasted_iota(jnp.int32, (tokens, WIN), 1)
        for b in range(n):
            for e in range(own):
                i = b * own + e
                hit = pos_ref[:, i : i + 1] == lane
                mix_ref[b, :, e * WIN : (e + 1) * WIN] = jnp.where(hit, gate_ref[:, i : i + 1], 0.0).astype(BF16)
        meet(barrier, (partner, beside_y, beside_x))

    def project(e):
        out_ref[j % 4, e, : 2 * WIN, :] = dot(here_ref[e], w_ref[e]).astype(BF16)
        step = (rows - 2 * WIN) // 2
        for r in (0, step):
            at = 2 * WIN + r
            out_ref[j % 4, e, at : at + step, :] = dot(away_ref[e, r : r + step, :], w_ref[e]).astype(BF16)

    @pl.when(j < tiles)
    def _():
        for e in range(3):
            project(e)

    @pl.when((j >= 1) & (j <= tiles))
    def _():
        i = j - 1
        pair(i).wait_recv()

        @pl.when(i >= 2)
        def _():
            far(i - 2, 0).wait_send()
            far(i - 2, 1).wait_send()

        total = (term(i, 6) + pair_in[i % 6, 3].astype(F32)).astype(BF16)
        far_out[i % 2, 0] = total[:half]
        far_out[i % 2, 1] = total[half:]
        far(i, 0).start()
        far(i, 1).start()

    @pl.when((j >= 2) & (j <= tiles + 1))
    def _():
        i = j - 2
        far(i, 0).wait_recv()
        far(i, 1).wait_recv()

        @pl.when(i >= 2)
        def _():
            near(i - 2, 0).wait_send()
            near(i - 2, 1).wait_send()

        total = term(i, 4) + pair_in[i % 6, 2].astype(F32)
        near_out[i % 2, 0, :half] = total[:half].astype(BF16)
        near_out[i % 2, 0, half:] = (total[half:] + far_in[i % 4, 1].astype(F32)).astype(BF16)
        near(i, 0).start()
        total = term(i, 2) + pair_in[i % 6, 1].astype(F32)
        near_out[i % 2, 1, :half] = (total[:half] + far_in[i % 4, 0].astype(F32)).astype(BF16)
        near_out[i % 2, 1, half:] = total[half:].astype(BF16)
        near(i, 1).start()

    @pl.when(j >= 3)
    def _():
        i = j - 3
        total = dot(hs_ref[...], s_ref[...]) + term(i, 0) + pair_in[i % 6, 0].astype(F32)
        near(i, 0).wait_recv()
        near(i, 1).wait_recv()
        total = total + near_in[i % 4, 0].astype(F32) + near_in[i % 4, 1].astype(F32)
        y_ref[...] = total.astype(BF16)

    @pl.when(j < tiles)
    def _():
        for e in range(3, own):
            project(e)

        @pl.when(j >= 2)
        def _():
            pair(j - 2).wait_send()

        for q in range(n // 2):
            pair_out[j % 2, q] = term(j, 2 * q + 1).astype(BF16)
        pair(j).start()

    @pl.when(j == tiles + 2)
    def _():
        for i in (tiles - 2, tiles - 1):
            pair(i).wait_send()
            for k in range(2):
                far(i, k).wait_send()
                near(i, k).wait_send()


def down(here, away, hs, w_down, s_down, pos, gate, tile):
    own, _, ff = here.shape
    n = pos.shape[1] // own
    rows = n * WIN
    tokens, depth = pos.shape[0], w_down.shape[2]
    tiles = depth // tile
    half = tokens // 2
    one = pl.Buffered(1)

    def whole(v):
        return pl.BlockSpec(v.shape, lambda j: (0,) * v.ndim, pipeline_mode=one)

    flops = 2 * own * rows * ff * depth
    dma = pltpu.SemaphoreType.DMA
    return pl.pallas_call(
        functools.partial(down_kernel, n, own, tiles),
        out_shape=jax.ShapeDtypeStruct((tokens, depth), BF16),
        grid=(tiles + 3,),
        in_specs=[
            whole(pos),
            whole(gate),
            whole(here),
            whole(away),
            whole(hs),
            pl.BlockSpec((own, ff, tile), lambda j: (0, 0, jnp.minimum(j, tiles - 1))),
            pl.BlockSpec((s_down.shape[0], tile), lambda j: (0, jnp.maximum(j - 3, 0))),
        ],
        out_specs=pl.BlockSpec((tokens, tile), lambda j: (0, jnp.maximum(j - 3, 0))),
        scratch_shapes=[
            pltpu.VMEM((4, own, rows, tile), BF16),
            pltpu.VMEM((n, tokens, own * WIN), BF16),
            pltpu.VMEM((2, n // 2, tokens, tile), BF16),
            pltpu.VMEM((6, n // 2, tokens, tile), BF16),
            pltpu.VMEM((2, 2, half, tile), BF16),
            pltpu.VMEM((4, 2, half, tile), BF16),
            pltpu.VMEM((2, 2, tokens, tile), BF16),
            pltpu.VMEM((4, 2, tokens, tile), BF16),
            dma((2,)),
            dma((6,)),
            dma((2, 2)),
            dma((4, 2)),
            dma((2, 2)),
            dma((4, 2)),
        ],
        compiler_params=pltpu.CompilerParams(
            vmem_limit_bytes=VMEM_LIMIT, collective_id=0, has_side_effects=True
        ),
        cost_estimate=pl.CostEstimate(flops=flops, bytes_accessed=own * ff * depth * 2, transcendentals=0),
        name="down",
    )(pos, gate, here, away, hs, w_down, s_down)


def solution(mesh):
    n = mesh.shape["ep"]

    def local(x, expert, slot, gate, w_gate, w_up, w_down, s_gate, s_up, s_down):
        x, expert, slot, gate = x[0, 0], expert[0, 0], slot[0, 0], gate[0, 0]
        tokens, top = expert.shape
        own = w_gate.shape[0]
        experts = own * n
        slots = 5 * tokens * top // (4 * experts)

        hit = (expert[:, :, None] == jnp.arange(experts)) & (slot < slots)[:, :, None]
        pos = jnp.sum(jnp.where(hit, slot[:, :, None] + 1, 0), axis=1) - 1
        weight = jnp.sum(jnp.where(hit, gate.astype(BF16).astype(F32)[:, :, None], 0.0), axis=1)
        note = jnp.stack([pos.astype(F32), weight]).reshape(2, tokens, n, own).transpose(2, 0, 3, 1)
        note = jnp.pad(note.reshape(n, 2 * own, tokens), ((0, 0), (0, 8 - 2 * own), (0, 0)))
        hs, here, away, notes = up(x, note, s_gate, s_up, w_gate, w_up)
        pos_col = notes[:, :own].reshape(n * own, tokens).T.astype(jnp.int32)
        weight = notes[:, own : 2 * own].reshape(n * own, tokens).T
        y = down(here, away, hs, w_down, s_down, pos_col, weight, 512)
        return y[None, None]

    tok, exp, rep = P("dp", "ep"), P("ep"), P()
    return jax.shard_map(
        local,
        mesh=mesh,
        in_specs=(tok, tok, tok, tok, exp, exp, exp, rep, rep, rep),
        out_specs=tok,
        check_vma=False,
    )
```

time: 432 us -> 391 us (0.905)
  Pallas kernels: 405 us -> 380 us
  blocking collectives: 15.3 us -> 0 us
    pallas_call x2 -> x1, Pallas kernels: 256 us -> 230 us  [up(): pl.pallas_call(functools.partial(up_kernel, own, n, (shared, pairs, rest,...]
    all_gather x1 -> x0, blocking collectives: 15.3 us -> none  [local(): lax.all_gather(jnp.concatenate([pos.astype(F32), weight], axis=1), 'ep')]
where the time goes in v2:
time: 391 us
  Pallas kernels  380 us (97%)
  local copies, waits for them, and re-layouts  6.33 us (2%)
  other arithmetic  4.54 us (1%)
    pallas_call x1, Pallas kernels, up(): pl.pallas_call(functools.partial(up_kernel, own, n, (shared, pairs, rest,...  230 us
    pallas_call x1, Pallas kernels, down(): pl.pallas_call(functools.partial(down_kernel, n, own, tiles), out_shape=j...  150 us

profile of v2, /device:TPU:0, one launch (start us, length us, event | category | flops | bytes accessed | tf_op | source)
XLA Modules:
  0.0 390.8 jit_solution(8608977184544749278)
XLA Ops:
  0.0 0.7 compare_bitcast_fusion
  0.7 0.7 bitcast_convert_fusion
  1.4 0.7 add_bitcast_fusion
  2.1 0.7 select_reduce_fusion.1
  2.9 0.7 select_reduce_fusion
  3.7 0.6 pad.4.note_ref
  4.4 229.9 %up.1 = (bf16[256,2048]{1,0:T(8,128)(2,1)}, bf16[3,224,2048]{2,1,0:T(8,128)(2,1)}, bf16[3,672,2048]{2,1,0:T(8,128)(2,1)}, f32[8,8,256]{2,1,0:T(8,128)}, bf16[6,2...) custom-call(f32[8,8,256]{2,1,0:T(8,128)} %pad.4.note_ref, bf16[256,7168]{1,0:T(8,128)(2,1)} %bitcast.25, ...), custom_call_target="tpu_custom_call" | custom-call | flops 172872433664 | bytes 352321536 | tf_op jit(solution)/shard_map/up/pallas_call | solution.py:315
  234.3 0.9 fusion.1
  235.3 0.8 copy.27
  236.0 0.7 copy.28
  236.8 149.9 %down.1 = bf16[256,7168]{1,0:T(8,128)(2,1)} custom-call(s32[256,24]{1,0:T(8,128)} %bitcast.21, f32[256,24]{1,0:T(8,128)} %bitcast.22, bf16[3,224,2048]{2,1,0:T(8,128)(2,1)} %get-tuple-element.10.here_ref, bf16[3,672,2048]{2,1,0:T(8,128)(2,1)} %get-tuple-element.11.away_ref, bf16[256,2048]{1,0:T(8,128)(2,1)} %get-tuple-element.12.hs_ref, ...), custom_call_target="tpu_custom_call" | custom-call | flops 78920024064 | bytes 88080384 | tf_op jit(solution)/shard_map/down/pallas_call | solution.py:491
  386.7 4.1 %copy.30 = bf16[1,1,256,7168]{3,2,1,0:T(8,128)(2,1)} copy(bf16[1,1,256,7168]{3,2,1,0:T(8,128)(2,1)} %bitcast.19) | data formatting | bytes 7340032
  (8 shorter events, 0.1 us)

commit v3 on v2

--- a/solution.py
+++ b/solution.py
@@ -16,6 +16,12 @@
 
 def dot(a, b):
     return lax.dot_general(a, b, (((a.ndim - 1,), (b.ndim - 2,)), ((), ())), preferred_element_type=F32)
+
+
+def window(q, slots):
+    first = q * slots // 16 * 16
+    shift = q * slots - first
+    return first, shift, (shift + slots + 15) // 16 * 16
 
 
 def remote(src, dst, left, here, device):
@@ -47,7 +53,7 @@
     pl.semaphore_wait(barrier, len(devices))
 
 
-def up_kernel(own, n, plan, note_ref, x_ref, sg_ref, su_ref, wg_ref, wu_ref, *refs):
+def up_kernel(own, n, slots, plan, note_ref, x_ref, sg_ref, su_ref, wg_ref, wu_ref, *refs):
     hs_ref, here_ref, away_ref, out_ref, far_ref, acc_ref = refs[:6]
     ring_ref, notes_ref, xp_ref, xr_ref, zp_ref, zr_ref, ga_ref, ua_ref, wide_ref = refs[6:15]
     note_left, note_here, pair_left, pair_here, left, here, ring_sem, load_sem, acc_sem = refs[15:]
@@ -205,8 +211,8 @@
         @pl.when(p % (2 * per) == 0)
         def _():
             e = p // (2 * per)
-            dispatch(notes_ref, 0, e, x_ref, zp_ref, 0)
-            dispatch(notes_ref, 1, e, xp_ref, zp_ref, WIN)
+            dispatch(notes_ref, 0, e, x_ref, zp_ref, (0, 0, WIN))
+            dispatch(notes_ref, 1, e, xp_ref, zp_ref, (WIN, 0, WIN))
 
         def store(v):
             here_ref[0] = v
@@ -237,7 +243,7 @@
         @pl.when(r % per == 0)
         def _():
             for q in range(n - 2):
-                dispatch(notes_ref, q + 2, r // per, xr_ref.at[q], zr_ref, q * WIN)
+                dispatch(notes_ref, q + 2, r // per, xr_ref.at[q], zr_ref, window(q, slots))
 
         rows = zr_ref.shape[0] // 2
 
@@ -280,14 +286,22 @@
 
 
 def dispatch(notes_ref, b, e, x_ref, z_ref, at):
+    first, shift, rows = at
     pos = notes_ref[b, pl.ds(e, 1), :]
-    slot = lax.broadcasted_iota(jnp.int32, (WIN, pos.shape[1]), 0).astype(F32)
-    hot = (slot == pos).astype(F32).astype(BF16)
+    pos = jnp.where(pos < 0, -1.0, pos + shift)
+    row = lax.broadcasted_iota(jnp.int32, (rows, pos.shape[1]), 0).astype(F32)
+    hot = (row == pos).astype(F32).astype(BF16)
     for k in range(0, z_ref.shape[1], 512):
-        z_ref[at : at + WIN, k : k + 512] = dot(hot, x_ref[:, k : k + 512]).astype(BF16)
-
-
-def up(x, note, s_gate, s_up, w_gate, w_up):
+        cols = slice(k, k + 512)
+        got = dot(hot, x_ref[:, cols])
+        if shift:
+            z_ref[first : first + 16, cols] = (got[:16] + z_ref[first : first + 16, cols].astype(F32)).astype(BF16)
+            z_ref[first + 16 : first + rows, cols] = got[16:].astype(BF16)
+        else:
+            z_ref[first : first + rows, cols] = got.astype(BF16)
+
+
+def up(x, note, slots, s_gate, s_up, w_gate, w_up):
     tokens, depth = x.shape
     own, _, ff = w_gate.shape
     n = note.shape[0]
@@ -295,7 +309,8 @@
     per = ff // TILE
     shared, pairs, rest = 2 * s_gate.shape[1] // TILE, 2 * own * per, own * per
     late = shared + pairs
-    rows = (n - 2) * WIN
+    rows = (n - 2) * slots
+    rows = (rows + 31) // 32 * 32
     one = pl.Buffered(1)
 
     def whole(v):
@@ -313,7 +328,7 @@
     dma = pltpu.SemaphoreType.DMA
     flops = 4 * (tokens * s_gate.shape[1] + own * (2 * WIN + rows) * ff) * depth
     return pl.pallas_call(
-        functools.partial(up_kernel, own, n, (shared, pairs, rest, per)),
+        functools.partial(up_kernel, own, n, slots, (shared, pairs, rest, per)),
         out_shape=(
             jax.ShapeDtypeStruct((tokens, s_gate.shape[1]), BF16),
             jax.ShapeDtypeStruct((own, 2 * WIN, ff), BF16),
@@ -360,9 +375,9 @@
     )(note, x, s_gate, s_up, w_gate, w_up)[:4]
 
 
-def down_kernel(n, own, tiles, pos_ref, gate_ref, here_ref, away_ref, hs_ref, w_ref, s_ref, y_ref, out_ref, mix_ref, *bufs):
+def down_kernel(n, own, slots, tiles, pos_ref, gate_ref, here_ref, away_ref, hs_ref, w_ref, s_ref, y_ref, h_ref, out_ref, mix_ref, *bufs):
     pair_out, pair_in, far_out, far_in, near_out, near_in = bufs[:6]
-    pair_left, pair_here, far_left, far_here, near_left, near_here = bufs[6:]
+    pair_left, pair_here, far_left, far_here, near_left, near_here, h_sem = bufs[6:]
     tokens = pos_ref.shape[0]
     rows = out_ref.shape[2]
     half = tokens // 2
@@ -382,25 +397,46 @@
         return remote(part, near_in.at[i % 4, k], near_left.at[i % 2, k], near_here.at[i % 4, k], (beside_x, beside_y)[k])
 
     def term(i, b):
-        seen = [out_ref[i % 4, e, b * WIN : (b + 1) * WIN, :] for e in range(own)]
-        return dot(mix_ref[b], jnp.concatenate(seen, axis=0))
+        first, _, size = seat(b)
+        seen = [out_ref[i % 4, e, first : first + size, :] for e in range(own)]
+        return dot(mix_ref[b, :, : own * size], jnp.concatenate(seen, axis=0))
+
+    def seat(b):
+        if b < 2:
+            return b * WIN, 0, WIN
+        first, shift, size = window(b - 2, slots)
+        return 2 * WIN + first, shift, size
+
+    def parts(e):
+        return (
+            pltpu.make_async_copy(here_ref.at[e], h_ref.at[e, pl.ds(0, 2 * WIN)], h_sem.at[e, 0]),
+            pltpu.make_async_copy(away_ref.at[e], h_ref.at[e, pl.ds(2 * WIN, rows - 2 * WIN)], h_sem.at[e, 1]),
+        )
 
     @pl.when(j == 0)
     def _():
-        lane = lax.broadcasted_iota(jnp.int32, (tokens, WIN), 1)
+        for e in range(own):
+            for part in parts(e):
+                part.start()
         for b in range(n):
+            _, shift, size = seat(b)
+            lane = lax.broadcasted_iota(jnp.int32, (tokens, size), 1)
             for e in range(own):
                 i = b * own + e
-                hit = pos_ref[:, i : i + 1] == lane
-                mix_ref[b, :, e * WIN : (e + 1) * WIN] = jnp.where(hit, gate_ref[:, i : i + 1], 0.0).astype(BF16)
+                pos = pos_ref[:, i : i + 1]
+                hit = jnp.where(pos < 0, -1, pos + shift) == lane
+                mix_ref[b, :, e * size : (e + 1) * size] = jnp.where(hit, gate_ref[:, i : i + 1], 0.0).astype(BF16)
         meet(barrier, (partner, beside_y, beside_x))
 
     def project(e):
-        out_ref[j % 4, e, : 2 * WIN, :] = dot(here_ref[e], w_ref[e]).astype(BF16)
-        step = (rows - 2 * WIN) // 2
+        @pl.when(j == 0)
+        def _():
+            for part in parts(e):
+                part.wait()
+
+        step = rows // 2
         for r in (0, step):
-            at = 2 * WIN + r
-            out_ref[j % 4, e, at : at + step, :] = dot(away_ref[e, r : r + step, :], w_ref[e]).astype(BF16)
+            out_ref[j % 4, e, r : r + step, :] = dot(h_ref[e, r : r + step, :], w_ref[e]).astype(BF16)
 
     @pl.when(j < tiles)
     def _():
@@ -474,10 +510,10 @@
                 near(i, k).wait_send()
 
 
-def down(here, away, hs, w_down, s_down, pos, gate, tile):
+def down(here, away, slots, hs, w_down, s_down, pos, gate, tile):
     own, _, ff = here.shape
     n = pos.shape[1] // own
-    rows = n * WIN
+    rows = 2 * WIN + away.shape[1]
     tokens, depth = pos.shape[0], w_down.shape[2]
     tiles = depth // tile
     half = tokens // 2
@@ -489,22 +525,23 @@
     flops = 2 * own * rows * ff * depth
     dma = pltpu.SemaphoreType.DMA
     return pl.pallas_call(
-        functools.partial(down_kernel, n, own, tiles),
+        functools.partial(down_kernel, n, own, slots, tiles),
         out_shape=jax.ShapeDtypeStruct((tokens, depth), BF16),
         grid=(tiles + 3,),
         in_specs=[
             whole(pos),
             whole(gate),
-            whole(here),
-            whole(away),
+            pl.BlockSpec(memory_space=pl.ANY),
+            pl.BlockSpec(memory_space=pl.ANY),
             whole(hs),
             pl.BlockSpec((own, ff, tile), lambda j: (0, 0, jnp.minimum(j, tiles - 1))),
             pl.BlockSpec((s_down.shape[0], tile), lambda j: (0, jnp.maximum(j - 3, 0))),
         ],
         out_specs=pl.BlockSpec((tokens, tile), lambda j: (0, jnp.maximum(j - 3, 0))),
         scratch_shapes=[
+            pltpu.VMEM((own, rows, ff), BF16),
             pltpu.VMEM((4, own, rows, tile), BF16),
-            pltpu.VMEM((n, tokens, own * WIN), BF16),
+            pltpu.VMEM((n, tokens, own * 128), BF16),
             pltpu.VMEM((2, n // 2, tokens, tile), BF16),
             pltpu.VMEM((6, n // 2, tokens, tile), BF16),
             pltpu.VMEM((2, 2, half, tile), BF16),
@@ -517,6 +554,7 @@
             dma((4, 2)),
             dma((2, 2)),
             dma((4, 2)),
+            dma((own, 2)),
         ],
         compiler_params=pltpu.CompilerParams(
             vmem_limit_bytes=VMEM_LIMIT, collective_id=0, has_side_effects=True
@@ -541,10 +579,10 @@
         weight = jnp.sum(jnp.where(hit, gate.astype(BF16).astype(F32)[:, :, None], 0.0), axis=1)
         note = jnp.stack([pos.astype(F32), weight]).reshape(2, tokens, n, own).transpose(2, 0, 3, 1)
         note = jnp.pad(note.reshape(n, 2 * own, tokens), ((0, 0), (0, 8 - 2 * own), (0, 0)))
-        hs, here, away, notes = up(x, note, s_gate, s_up, w_gate, w_up)
+        hs, here, away, notes = up(x, note, slots, s_gate, s_up, w_gate, w_up)
         pos_col = notes[:, :own].reshape(n * own, tokens).T.astype(jnp.int32)
         weight = notes[:, own : 2 * own].reshape(n * own, tokens).T
-        y = down(here, away, hs, w_down, s_down, pos_col, weight, 512)
+        y = down(here, away, slots, hs, w_down, s_down, pos_col, weight, 512)
         return y[None, None]
 
     tok, exp, rep = P("dp", "ep"), P("ep"), P()

time: 391 us -> 383 us (0.980)
  Pallas kernels: 380 us -> 372 us
    pallas_call x2, Pallas kernels: 380 us -> 372 us  [the longest x1 224 us: up(): pl.pallas_call(functools.partial(up_kernel, own, n, slots, (shared, pairs...]
where the time goes in v3:
time: 383 us
  Pallas kernels  372 us (97%)
  local copies, waits for them, and re-layouts  6.33 us (2%)
  other arithmetic  4.54 us (1%)
    pallas_call x1, Pallas kernels, up(): pl.pallas_call(functools.partial(up_kernel, own, n, slots, (shared, pairs...  224 us
    pallas_call x1, Pallas kernels, down(): pl.pallas_call(functools.partial(down_kernel, n, own, slots, tiles), out_...  148 us

profile of v3, /device:TPU:0, one launch (start us, length us, event | category | flops | bytes accessed | tf_op | source)
XLA Modules:
  0.0 382.8 jit_solution(13303973048742416876)
XLA Ops:
  0.0 0.7 compare_bitcast_fusion
  0.7 0.7 bitcast_convert_fusion
  1.4 0.7 add_bitcast_fusion
  2.1 0.7 select_reduce_fusion.1
  2.9 0.7 select_reduce_fusion
  3.7 0.6 pad.4.note_ref
  4.4 223.9 %up.1 = (bf16[256,2048]{1,0:T(8,128)(2,1)}, bf16[3,224,2048]{2,1,0:T(8,128)(2,1)}, bf16[3,640,2048]{2,1,0:T(8,128)(2,1)}, f32[8,8,256]{2,1,0:T(8,128)}, bf16[6,2...) custom-call(f32[8,8,256]{2,1,0:T(8,128)} %pad.4.note_ref, bf16[256,7168]{1,0:T(8,128)(2,1)} %bitcast.25, ...), custom_call_target="tpu_custom_call" | custom-call | flops 167235289088 | bytes 352321536 | tf_op jit(solution)/shard_map/up/pallas_call | solution.py:330
  228.3 0.9 fusion.1
  229.2 0.8 copy.27
  230.0 0.7 copy.28
  230.7 147.9 %down.1 = bf16[256,7168]{1,0:T(8,128)(2,1)} custom-call(s32[256,24]{1,0:T(8,128)} %bitcast.21, f32[256,24]{1,0:T(8,128)} %bitcast.22, bf16[3,224,2048]{2,1,0:T(8,128)(2,1)} %get-tuple-element.10.here_ref, bf16[3,640,2048]{2,1,0:T(8,128)(2,1)} %get-tuple-element.11.away_ref, bf16[256,2048]{1,0:T(8,128)(2,1)} %get-tuple-element.12.hs_ref, ...), custom_call_target="tpu_custom_call" | custom-call | flops 76101451776 | bytes 88080384 | tf_op jit(solution)/shard_map/down/pallas_call | solution.py:527
  378.6 4.1 %copy.30 = bf16[1,1,256,7168]{3,2,1,0:T(8,128)(2,1)} copy(bf16[1,1,256,7168]{3,2,1,0:T(8,128)(2,1)} %bitcast.19) | data formatting | bytes 7340032
  (8 shorter events, 0.1 us)
